TPU v7x, 256 devices: a 8x8x2 block of a 8x8x16 slice. The times are simulated.
256 devices in a mesh: groups: 2 (over z), expert: 64 (over y, x), tensor: 2 (over core).
Axes of the slice: x: 8, y: 8, z: 2, core: 2. Of those that a mesh axis runs over, the one named last changes fastest.
The devices are a block of a 8x8x16 slice.
Arguments:
- tokens: bfloat16 [1024, 6144], P(('groups', 'expert')), parts along dimension 0, may hold values from -6 to 6
- routes: int32 [1024, 2], P(('groups', 'expert')), parts along dimension 0, may hold values from 0 to 3, all different within a row; in each aligned block of 8 rows (0 to 7, 8 to 15, ...) at most 5 rows name the same one
- router_logits: float32 [1024, 4], P(('groups', 'expert')), parts along dimension 0, may hold values from -9 to 310
- gate_weight: bfloat16 [64, 6144, 512], P('expert', None, 'tensor'), may hold values from -0.078125 to 0.078125
- up_weight: bfloat16 [64, 6144, 512], P('expert', None, 'tensor'), may hold values from -0.078125 to 0.078125
- down_weight: bfloat16 [64, 512, 6144], P('expert', 'tensor'), may hold values from -0.0625 to 0.0625
Outputs:
- layer_out: bfloat16 [1024, 6144], P(('groups', 'expert'), 'tensor'), parts along dimension 0
There are 2 independent parts, one for each index of `groups`. A program takes and returns all parts, laid end to end along the dimension named above; an argument that names none is the same for every part. Nothing has to cross between parts.
Inputs may be any that keep to these rules, and one draw needn't show every extreme that they name: `routes`: each row names two different experts. In the rows of one index of expert (aligned blocks of 8 rows) no expert is named more than 5 times, and in every draw some block names some expert exactly 5 times.
All inputs are finite; a program needn't handle non-finite values.
Results may differ from a plain program's by a relative error of at most 0.0049.
Values may be sent and summed in bfloat16 or wider, within the bound.
A program may use at most 64 MiB of HBM per device.

v0:
```python
import jax
import jax.numpy as jnp
from jax import lax
from jax.sharding import PartitionSpec as P

CAP = 5


def in_blocks(value, dim, devices):
    shape = value.shape
    blocks = value.reshape(*shape[:dim], devices, shape[dim] // devices, *shape[dim + 1 :])
    return jnp.moveaxis(blocks, dim, 0)


def sent_and_summed(value, axis, dim):
    blocks = in_blocks(value, dim, lax.axis_size(axis))
    arrived = lax.all_to_all(blocks, axis, split_axis=0, concat_axis=0, tiled=True)
    return arrived.sum(axis=0)


def piece_ends(length, count):
    lap = length // count
    if lap >= 8:
        lap -= lap % 8
    return [lap * k for k in range(1, count)]


def joined_along(blocks, dim):
    blocks = jnp.moveaxis(blocks, 0, dim)
    shape = blocks.shape
    return blocks.reshape(*shape[:dim], shape[dim] * shape[dim + 1], *shape[dim + 2 :])


def exchange_in_pieces(value, axis, pieces, split_dim, concat_dim):
    blocks = in_blocks(value, split_dim, lax.axis_size(axis))
    widest = max(range(1, max(2, blocks.ndim - 1)), key=lambda d: blocks.shape[d])
    finished = []
    for share in jnp.split(blocks, piece_ends(blocks.shape[widest], pieces), axis=widest):
        if share.size:
            finished.append(lax.all_to_all(share, axis, split_axis=0, concat_axis=0, tiled=True))
    return joined_along(jnp.concatenate(finished, axis=widest), concat_dim)


def shards(tokens, routes, router_logits, gate_weight, up_weight, down_weight):
    local_tokens = tokens.shape[0]
    width = tokens.shape[1]
    experts = router_logits.shape[1]
    devices = lax.axis_size("expert")
    segments = devices // experts
    capacity = CAP
    expert_ids = jnp.arange(experts, dtype=jnp.int32)
    picked = jnp.take_along_axis(router_logits, routes, axis=1)
    route_weight = jax.nn.softmax(picked, axis=1)
    onehot = (routes[:, :, None] == expert_ids[None, None, :]).astype(jnp.int32)
    flat_hot = onehot.reshape(local_tokens * 2, experts)
    earlier = jnp.cumsum(flat_hot, axis=0) - flat_hot
    slot_index = jnp.sum(earlier * flat_hot, axis=1).reshape(local_tokens, 2)
    target = routes * capacity + slot_index
    cell_ids = jnp.arange(experts * capacity, dtype=jnp.int32)
    placed = target[:, :, None] == cell_ids[None, None, :]
    pick_matrix = jnp.any(placed, axis=1).astype(jnp.bfloat16)
    mix_matrix = jnp.sum(route_weight[:, :, None] * placed.astype(jnp.float32), axis=1)
    buffer = jnp.einsum(
        "tc,td->cd", pick_matrix, tokens, preferred_element_type=jnp.float32
    ).astype(jnp.bfloat16)
    buffer = buffer.reshape(experts, capacity, width)
    gate_local = gate_weight[0]
    up_local = up_weight[0]
    down_local = down_weight[0]
    outgoing = jnp.repeat(buffer, segments, axis=0)
    half_width = width // lax.axis_size("tensor")
    own_columns = lax.dynamic_slice_in_dim(
        outgoing, lax.axis_index("tensor") * half_width, half_width, 2
    )
    slot_rows = lax.all_gather(
        lax.all_to_all(own_columns, "expert", split_axis=0, concat_axis=0, tiled=True),
        "tensor",
        axis=2,
        tiled=True,
    )
    sources = slot_rows.shape[0]
    items = slot_rows.shape[1]
    flattened = slot_rows.reshape(sources * items, slot_rows.shape[2])
    gate_out = jnp.dot(flattened, gate_local, preferred_element_type=jnp.float32)
    up_out = jnp.dot(flattened, up_local, preferred_element_type=jnp.float32)
    hidden = (jax.nn.silu(gate_out) * up_out).astype(jnp.bfloat16)
    result = jnp.dot(hidden, down_local, preferred_element_type=jnp.float32)
    partial_out = result.reshape(sources, items, width)
    reduced = sent_and_summed(partial_out, "tensor", 2)
    returned = exchange_in_pieces(reduced, "expert", 2, 0, 0)
    columns_here = returned.shape[2]
    gathered_out = jnp.sum(returned.reshape(experts, segments, capacity, columns_here), axis=1)
    gathered_out = gathered_out.reshape(experts * capacity, columns_here)
    layer_out = jnp.dot(
        mix_matrix,
        gathered_out,
        precision=lax.Precision.HIGHEST,
        preferred_element_type=jnp.float32,
    )
    return layer_out.astype(jnp.bfloat16)


def solution(mesh):
    return jax.shard_map(
        shards,
        mesh=mesh,
        in_specs=(
            P(("groups", "expert"), None),
            P(("groups", "expert"), None),
            P(("groups", "expert"), None),
            P("expert", None, "tensor"),
            P("expert", None, "tensor"),
            P("expert", "tensor", None),
        ),
        out_specs=P(("groups", "expert"), "tensor"),
        check_vma=False,
    )
```

profile of v0, /device:TPU:513, one launch (start us, length us, event | category | flops | bytes accessed | tf_op | source)
XLA Modules:
  0.0 311.8 jit_solution(12775214072166252372)
XLA Ops:
  8.1 1.9 convolution_convert_fusion
  10.0 1.1 reshape.56
  12.1 88.7 %all_to_all.20 = bf16[64,5,3072]{2,1,0:T(8,128)(2,1)} all-to-all(bf16[64,5,3072]{2,1,0:T(8,128)(2,1)S(1)} %constant_dynamic-slice_fusion), channel_id=1, replica_groups=mesh['groups'=2,'expert'=64,'tensor'=2] {'expert'}, dimensions={0} | all-to-all | bytes 3932160 | tf_op jit(solution)/shard_map/all_to_all | solution.py:76
  100.8 4.7 %copy.91 = bf16[6144,256]{1,0:T(8,128)(2,1)} copy(bf16[6144,256]{0,1:T(8,128)(2,1)} %bitcast.38) | data formatting | bytes 6291456 | tf_op jit(solution)/shard_map/dot_general | solution.py:87
  105.6 35.1 %all-gather.2.cloned.1.call-done = bf16[64,5,6144]{2,1,0:T(8,128)(2,1)} async-done(((bf16[64,5,3072]{2,1,0:T(8,128)(2,1)}), bf16[64,5,6144]{2,1,0:T(8,128)(2,1)}) %all-gather.2.cloned.1.call-update) | async-done | bytes 3932176 | tf_op jit(solution)/shard_map/all_gather | solution.py:75
  140.6 7.7 %reshape.58 = bf16[320,6144]{1,0:T(8,128)(2,1)} reshape(bf16[64,5,6144]{2,1,0:T(8,128)(2,1)} %all-gather.2.cloned.1.call-done) | data formatting | bytes 7864320 | tf_op jit(solution)/shard_map/reshape | solution.py:83
  148.3 3.4 %fusion.2 = f32[320,256]{1,0:T(8,128)S(1)} fusion(bf16[320,6144]{1,0:T(8,128)(2,1)} %reshape.58, bf16[1,6144,256]{2,1,0:T(8,128)(2,1)S(1)} %copy-done), kind=kOutput, calls=%fused_computation.7 | convolution fusion | flops 1006632960 | bytes 7405568 | tf_op jit(solution)/shard_map/dot_general | solution.py:84
  152.6 1.8 fusion.7
  155.4 1.2 convolution_bitcast_fusion
  157.6 11.2 %all_to_all.21 = f32[2,64,5,3072]{3,1,2,0:T(8,128)} all-to-all(f32[2,64,5,3072]{3,1,2,0:T(8,128)S(1)} %copy.81), channel_id=1, replica_groups=mesh['groups'=2,'expert'=64,'tensor'=2] {'tensor'}, dimensions={0} | all-to-all | bytes 15728640 | tf_op jit(solution)/shard_map/all_to_all | solution.py:17
  168.8 6.3 %reduce_sum.48 = f32[64,5,3072]{2,0,1:T(8,128)} reduce(f32[2,64,5,3072]{3,1,2,0:T(8,128)} %all_to_all.21, f32[]{:T(128)} %constant.36.clone.1), dimensions={0}, to_apply=%region_6.7 | reduce | flops 983040 | bytes 11796484 | tf_op jit(solution)/shard_map/reduce_sum | solution.py:18
  175.1 1.5 split.8
  176.6 2.4 copy.83
  179.0 13.4 %all-to-all-start.2 = ((f32[64,1,2,3072]{3,2,1,0:T(2,128)}), f32[64,1,2,3072]{3,2,1,0:T(2,128)}, u32[]{:S(2)}, u32[]{:S(2)}) async-start(f32[64,1,2,3072]{3,2,1,0:T(2,128)} %copy.83), calls=%async_computation.2 | async-start | bytes 3145728 | tf_op jit(solution)/shard_map/all_to_all | solution.py:40
  192.4 1.9 split.9
  194.3 3.8 %copy.84 = f32[64,1,3,3072]{3,1,2,0:T(1,128)} copy(f32[64,1,3,3072]{3,0,2,1:T(8,128)S(1)} %split.9) | data formatting | bytes 4718592 | tf_op jit(solution)/shard_map/split | solution.py:38
  198.1 32.4 %all-to-all-done.2 = f32[64,1,2,3072]{3,2,1,0:T(2,128)} async-done(((f32[64,1,2,3072]{3,2,1,0:T(2,128)}), f32[64,1,2,3072]{3,2,1,0:T(2,128)}, u32[]{:S(2)}, u32[]{:S(2)}) %all-to-all-start.2) | async-done | bytes 1572896 | tf_op jit(solution)/shard_map/all_to_all | solution.py:40
  230.5 10.0 %all-to-all-start.3 = ((f32[64,1,3,3072]{3,1,2,0:T(1,128)}), f32[64,1,3,3072]{3,1,2,0:T(1,128)S(1)}, u32[]{:S(2)}, u32[]{:S(2)}) async-start(f32[64,1,3,3072]{3,1,2,0:T(1,128)} %copy.84), calls=%async_computation.3 | async-start | bytes 4718592 | tf_op jit(solution)/shard_map/all_to_all | solution.py:40
  242.1 3.1 copy.85
  245.2 48.8 %all-to-all-done.3 = f32[64,1,3,3072]{3,1,2,0:T(1,128)S(1)} async-done(((f32[64,1,3,3072]{3,1,2,0:T(1,128)}), f32[64,1,3,3072]{3,1,2,0:T(1,128)S(1)}, u32[]{:S(2)}, u32[]{:S(2)}) %all-to-all-start.3) | async-done | bytes 2359328 | tf_op jit(solution)/shard_map/all_to_all | solution.py:40
  295.4 2.3 pad_maximum_fusion
  297.7 3.6 %reduce_sum.49 = f32[4,5,3072]{2,0,1:T(4,128)} reduce(f32[4,16,5,3072]{3,1,0,2:T(8,128)} %bitcast.35, f32[]{:T(128)} %constant.36.clone.1), dimensions={1}, to_apply=%region_7.8 | reduce | flops 921600 | bytes 4177924 | tf_op jit(solution)/shard_map/reduce_sum | solution.py:92
  301.3 1.1 copy.87
  303.1 1.9 convolution_convert_fusion.1
  (42 shorter events, 9.1 us)
Async XLA Ops:
  6.5 141.8 %copy-start = (bf16[1,6144,256]{2,1,0:T(8,128)(2,1)S(1)}, bf16[1,6144,256]{2,1,0:T(8,128)(2,1)}, u32[]{:S(2)}) copy-start(bf16[1,6144,256]{2,1,0:T(8,128)(2,1)} %param.9) | copy-start | bytes 9437188
  6.6 134.1 %all-gather.2.cloned.1.call-start = ((), (), s32[]{:S(2)}) async-start(), calls=%async_computation.4 | async-start | bytes 9437184 | tf_op jit(solution)/shard_map/all_gather | solution.py:75
  148.3 3.5 %copy-start.5 = (bf16[320,6144]{1,0:T(8,128)(2,1)S(1)}, bf16[320,6144]{1,0:T(8,128)(2,1)}, u32[]{:S(2)}) copy-start(bf16[320,6144]{1,0:T(8,128)(2,1)} %reshape.58) | copy-start | bytes 11796484
  148.3 4.3 %copy-start.6 = (bf16[1,6144,256]{2,1,0:T(8,128)(2,1)S(1)}, bf16[1,6144,256]{2,1,0:T(8,128)(2,1)}, u32[]{:S(2)}) copy-start(bf16[1,6144,256]{2,1,0:T(8,128)(2,1)} %param.10) | copy-start | bytes 9437188
  152.6 2.8 copy-start.3
  179.0 51.5 %all-to-all-start.2 = ((f32[64,1,2,3072]{3,2,1,0:T(2,128)}), f32[64,1,2,3072]{3,2,1,0:T(2,128)}, u32[]{:S(2)}, u32[]{:S(2)}) async-start(f32[64,1,2,3072]{3,2,1,0:T(2,128)} %copy.83), calls=%async_computation.2 | async-start | bytes 3145728 | tf_op jit(solution)/shard_map/all_to_all | solution.py:40
  198.1 42.6 %copy-start.2 = (f32[8,4]{0,1:T(4,128)S(1)}, f32[8,4]{0,1:T(4,128)}, u32[]{:S(2)}) copy-start(f32[8,4]{0,1:T(4,128)} %param.8) | copy-start | bytes 388
  230.5 63.4 %all-to-all-start.3 = ((f32[64,1,3,3072]{3,1,2,0:T(1,128)}), f32[64,1,3,3072]{3,1,2,0:T(1,128)S(1)}, u32[]{:S(2)}, u32[]{:S(2)}) async-start(f32[64,1,3,3072]{3,1,2,0:T(1,128)} %copy.84), calls=%async_computation.3 | async-start | bytes 4718592 | tf_op jit(solution)/shard_map/all_to_all | solution.py:40
  293.9 1.4 copy-start.4
  295.3 9.6 %copy-start.1 = (bf16[1,6144,256]{2,1,0:T(8,128)(2,1)S(1)}, bf16[1,6144,256]{2,1,0:T(8,128)(2,1)}, u32[]{:S(2)}) copy-start(bf16[1,6144,256]{2,1,0:T(8,128)(2,1)} %param.9) | copy-start | bytes 9437188
Sparse Core Ops, SparseCore 0:
  101.0 39.6 all-gather.1
where the time goes:
time: 315 us; the launch traced here: 312 us
  waiting for transfers between devices  116 us (37%)
  blocking collectives  99.9 us (32%)
  local copies, waits for them, and re-layouts  35.5 us (11%)
  starting transfers between devices  23.4 us (7%)
  between operations  13.6 us (4%)
  other arithmetic  13.1 us (4%)
  matrix products  10.2 us (3%)
    all_to_all x1, blocking collectives, shards(): lax.all_to_all(own_columns, 'expert', split_axis=0, concat_axis=0, tiled=...  88.7 us
    all_to_all x2, waiting for transfers between devices, exchange_in_pieces(): lax.all_to_all(share, axis, split_axis=0, concat_axis=0, tiled=True)  81.1 us
    all_gather x1, waiting for transfers between devices, shards(): lax.all_gather(lax.all_to_all(own_columns, 'expert', split_axis=0, concat...  35.1 us
    all_to_all x2, starting transfers between devices, exchange_in_pieces(): lax.all_to_all(share, axis, split_axis=0, concat_axis=0, tiled=True)  23.4 us
    all_to_all x1, blocking collectives, sent_and_summed(): lax.all_to_all(blocks, axis, split_axis=0, concat_axis=0, tiled=True)  11.2 us
    split x4, local copies, waits for them, and re-layouts, exchange_in_pieces(): jnp.split(blocks, piece_ends(blocks.shape[widest], pieces), axis=widest)  9.65 us
    reshape x1, local copies, waits for them, and re-layouts, shards(): flattened = slot_rows.reshape(sources * items, slot_rows.shape[2])  7.69 us
  transfers between devices with their start and end apart: 3, of which 3 were waited for; matrix products, arithmetic and copies ran while one was open for 5% of the time, Pallas kernels for 0%

commit v1 on v0

v1 whole, which is shorter than its diff:
```python
import functools
import math

import jax
import jax.numpy as jnp
from jax import lax
from jax.experimental import pallas as pl
from jax.experimental.pallas import tpu as pltpu
from jax.sharding import PartitionSpec as P

MESH = pl.DeviceIdType.MESH
F32, BF16 = jnp.float32, jnp.bfloat16
LANES = 128


def ring_order(side):
    order = [0]
    for k in range(1, side // 2):
        order += [k, side - k]
    return order + [side // 2]


def kernel(
    side, segs, tok, wrow, gate, up, down, out,
    gu, wd, own, sib, pre, hid, hmir, hsib, wall, wcol, part, csend, crecv, fsend, frecv,
    load_sem, p1_send, p1_recv, ring_send, ring_recv, d2d_send, d2d_recv,
    w1_send, w1_recv, w2_send, w2_recv, x_send, x_recv,
    cr_send, cr_recv, f_send, f_recv,
):
    order = ring_order(side)
    pos = {k: p for p, k in enumerate(order)}
    mirror = [pos[(side - k) % side] for k in order]
    cuts = [0, 1] + list(range(3, side - 2, 2)) + [side]
    blocks = list(zip(cuts[:-1], cuts[1:]))
    nb = len(blocks)
    rows, width = own.shape[3], own.shape[4]
    hc = wd.shape[1]
    hops = (side // 2, side // 2 - 1)

    core = lax.axis_index("tensor")
    place = lax.axis_index("expert")
    y, x = place // side, lax.rem(place, side)
    expert = place // segs
    sign = 1 - 2 * core

    def along(axis, k):
        step = sign * k + side
        if axis == 0:
            return {"expert": lax.rem(y + step, side) * side + x}
        return {"expert": y * side + lax.rem(x + step, side)}

    def remote(src, dst, send, recv, device):
        return pltpu.make_async_remote_copy(
            src_ref=src, dst_ref=dst, send_sem=send, recv_sem=recv, device_id=device, device_id_type=MESH
        )

    other = {"tensor": 1 - core}
    started = []

    def start(copy):
        copy.start()
        started.append(copy)

    def arrived(ref, send, recv):
        remote(ref, ref, send, recv, other).wait_recv()

    half = 2 * width
    tok_loads = [
        pltpu.make_async_copy(
            tok.at[:, pl.ds(pl.multiple_of(core * half + t * width, LANES), width)], own.at[t, 0, 0], load_sem.at[t]
        )
        for t in range(2)
    ]
    w_load = pltpu.make_async_copy(wrow, wall.at[0, 0], load_sem.at[2])
    for copy in tok_loads:
        copy.start()
    w_load.start()
    loads = []
    for q in range(4):
        who = core if q < 2 else 1 - core
        first = pl.multiple_of(who * half + (q % 2) * width, LANES)
        for i, matrix in enumerate((gate, up)):
            loads.append(
                pltpu.make_async_copy(
                    matrix.at[0, pl.ds(first, width), :], gu.at[q, :, pl.ds(i * hc, hc)], load_sem.at[4 + 2 * q + i]
                )
            )
    for copy in loads:
        copy.start()
    wd_load = pltpu.make_async_copy(
        down.at[0, :, pl.ds(pl.multiple_of(core * half, LANES), half)], wd.at[0], load_sem.at[3]
    )
    wd_load.start()

    barrier = pltpu.get_barrier_semaphore()
    for k in range(1, side):
        for axis in range(2):
            pl.semaphore_signal(barrier, inc=1, device_id=along(axis, k), device_id_type=MESH)
    pl.semaphore_signal(barrier, inc=1, device_id=other, device_id_type=MESH)
    pre[...] = jnp.zeros_like(pre)
    for copy in tok_loads:
        copy.wait()
    w_load.wait()
    pl.semaphore_wait(barrier, 2 * (side - 1) + 1)

    for k in order[1:]:
        back = pos[side - k]
        for t in range(2):
            start(remote(own.at[t, 0, 0], own.at[t, 0, back], p1_send.at[t, back], p1_recv.at[t, back], along(t, k)))
    def forward(t, d, h, b):
        lo, hi = blocks[b]
        k = (side - h) % side if d == 0 else h
        k_there = (side - h - 1) % side if d == 0 else h + 1
        start(remote(
            own.at[t, pos[k], lo:hi], own.at[t, pos[k_there], lo:hi],
            ring_send.at[t, d, h, b], ring_recv.at[t, pos[k_there], b], along(1 - t, 1 if d == 0 else side - 1),
        ))

    def project(src, t, q, chunk, mirrored):
        r = jnp.dot(src[t, chunk].reshape(side * rows, width), gu[q], preferred_element_type=F32)
        r = r.reshape(side, rows, 2 * hc)
        for p in range(side):
            at = (mirror[chunk], mirror[p]) if mirrored else (chunk, p)
            i, j = at if t == 0 else at[::-1]
            pre[i, j] += r[p]

    def own_dot(t, chunk):
        project(own, t, t, chunk, False)

    def sib_dot(t, chunk):
        arrived(sib.at[t, chunk], d2d_send.at[t, chunk], d2d_recv.at[t, chunk])
        project(sib, t, 2 + t, chunk, True)

    waiting = []
    loaded = False
    for step in range(side // 2 + nb):
        complete = []
        for h in reversed(range(side // 2 + 1)):
            b = step - h
            if b < 0 or b >= nb:
                continue
            lo, hi = blocks[b]
            for t in range(2):
                if h == 0:
                    for p in range(max(lo, 1), hi):
                        arrived(own.at[t, 0, p], p1_send.at[t, p], p1_recv.at[t, p])
                    for d in range(2):
                        forward(t, d, 0, b)
                    if b == nb - 1:
                        complete.append((t, 0))
                    continue
                for d in range(2):
                    if h > hops[d]:
                        continue
                    chunk = pos[(side - h) % side if d == 0 else h]
                    arrived(own.at[t, chunk, lo:hi], ring_send.at[t, 0, 0, b], ring_recv.at[t, chunk, b])
                    if h < hops[d]:
                        forward(t, d, h, b)
                    if b == nb - 1:
                        complete.append((t, chunk))
        for t, chunk in complete:
            start(remote(own.at[t, chunk], sib.at[t, chunk], d2d_send.at[t, chunk], d2d_recv.at[t, chunk], other))
        if step == 0:
            start(remote(
                down.at[0, :, pl.ds(pl.multiple_of((1 - core) * half, LANES), half)], wd.at[1],
                x_send.at[0], x_recv.at[0], other,
            ))
            for k in order[1:]:
                back = pos[side - k]
                start(remote(wall.at[0, 0], wall.at[0, back], w1_send.at[back], w1_recv.at[back], along(0, k)))
        if step == nb - 1:
            for p in range(1, side):
                arrived(wall.at[0, p], w1_send.at[p], w1_recv.at[p])
            for k in order[1:]:
                back = pos[side - k]
                start(remote(wall.at[0], wall.at[back], w2_send.at[back], w2_recv.at[back], along(1, k)))
        if (complete or waiting) and not loaded:
            for copy in loads:
                copy.wait()
            loaded = True
        for t, chunk in complete:
            own_dot(t, chunk)
        for t, chunk in waiting:
            sib_dot(t, chunk)
        waiting = complete
    for t, chunk in waiting:
        sib_dot(t, chunk)

    for i in range(side):
        g, u = pre[i, :, :, :hc], pre[i, :, :, hc:]
        h_here = (g / (1.0 + jnp.exp(-g)) * u).astype(BF16)
        hid[i] = h_here
        for j in range(side):
            hmir[mirror[i], mirror[j]] = h_here[j]
    start(remote(hmir, hsib, x_send.at[1], x_recv.at[1], other))

    for p in range(1, side):
        arrived(wall.at[p], w2_send.at[p], w2_recv.at[p])
    lane = lax.broadcasted_iota(jnp.int32, (side, rows, LANES), 2)
    row = lax.broadcasted_iota(jnp.int32, (side, rows, LANES), 1)
    for i in range(side):
        spread = jnp.broadcast_to(wall[i], (side, rows, LANES))
        wcol[i] = jnp.sum(jnp.where(lane == expert * rows + row, spread, 0.0), axis=2, keepdims=True)

    wd_load.wait()
    arrived(wd.at[1], x_send.at[0], x_recv.at[0])
    arrived(hsib, x_send.at[1], x_recv.at[1])

    def make_part(t, chunk):
        if t == 0:
            a, b, scale = hid[chunk], hsib[chunk], wcol[chunk]
        else:
            a, b, scale = hid[:, chunk], hsib[:, chunk], wcol[:, chunk]
        cols = slice(t * width, (t + 1) * width)
        r = jnp.dot(a.reshape(side * rows, hc), wd[0, :, cols], preferred_element_type=F32)
        r += jnp.dot(b.reshape(side * rows, hc), wd[1, :, cols], preferred_element_type=F32)
        part[t, chunk] = r.reshape(side, rows, width) * scale

    back_blocks = blocks[::-1]
    made = set()

    def need(t, k):
        if (t, k) not in made:
            made.add((t, k))
            make_part(t, pos[k])

    for step in range(side // 2 + nb):
        for h in reversed(range(side // 2 + 1)):
            b = step - h
            if b < 0 or b >= nb:
                continue
            lo, hi = back_blocks[b]
            for t in range(2):
                if h == side // 2:
                    need(t, 0)
                    arrived(crecv.at[t, 0, h, lo:hi], cr_send.at[t, 0, 0, b], cr_recv.at[t, 0, h, b])
                    arrived(crecv.at[t, 1, h - 1, lo:hi], cr_send.at[t, 0, 0, b], cr_recv.at[t, 1, h - 1, b])
                    total = (
                        part[t, 0, lo:hi]
                        + crecv[t, 0, h, lo:hi].astype(F32)
                        + crecv[t, 1, h - 1, lo:hi].astype(F32)
                    )
                    part[t, 0, lo:hi] = total
                    fsend[t, lo:hi] = total.astype(BF16)
                    for p in reversed(range(max(lo, 1), hi)):
                        k = order[p]
                        back = pos[side - k]
                        start(remote(fsend.at[t, p], frecv.at[t, back], f_send.at[t, back], f_recv.at[t, back], along(t, k)))
                    continue
                for d in range(2):
                    if h >= hops[d]:
                        continue
                    k = hops[d] - h if d == 0 else side - hops[d] + h
                    need(t, k)
                    value = part[t, pos[k], lo:hi]
                    if h > 0:
                        arrived(crecv.at[t, d, h, lo:hi], cr_send.at[t, 0, 0, b], cr_recv.at[t, d, h, b])
                        value = value + crecv[t, d, h, lo:hi].astype(F32)
                    csend[t, d, h, lo:hi] = value.astype(BF16)
                    start(remote(
                        csend.at[t, d, h, lo:hi], crecv.at[t, d, h + 1, lo:hi],
                        cr_send.at[t, d, h, b], cr_recv.at[t, d, h + 1, b], along(1 - t, 1 if d == 0 else side - 1),
                    ))
    for t in range(2):
        total = part[t, 0, 0]
        for p in range(1, side):
            arrived(frecv.at[t, p], f_send.at[t, p], f_recv.at[t, p])
            total = total + frecv[t, p].astype(F32)
        out[:, t * width:(t + 1) * width] = total.astype(out.dtype)
    for copy in started:
        copy.wait_send()


def solution(mesh):
    n_expert = mesh.shape["expert"]
    side = math.isqrt(n_expert)
    nb = len([0, 1] + list(range(3, side - 2, 2)))

    def layer(tokens, routes, router_logits, gate_weight, up_weight, down_weight):
        rows, width = tokens.shape[0], tokens.shape[1] // 4
        experts = router_logits.shape[1]
        hc = down_weight.shape[1]
        named = routes[:, :, None] == jnp.arange(experts, dtype=jnp.int32)
        picked = jnp.sum(jnp.where(named, router_logits[:, None, :], 0.0), axis=2)
        weight = jnp.sum(jnp.where(named, jax.nn.softmax(picked, axis=1)[:, :, None], 0.0), axis=1)
        wrow = jnp.pad(weight.T.reshape(1, experts * rows), ((0, 0), (0, LANES - experts * rows)))
        hop = side // 2
        dma = pltpu.SemaphoreType.DMA
        scratch = [
            pltpu.VMEM((4, width, 2 * hc), BF16),
            pltpu.VMEM((2, hc, 2 * width), BF16),
            pltpu.VMEM((2, side, side, rows, width), BF16),
            pltpu.VMEM((2, side, side, rows, width), BF16),
            pltpu.VMEM((side, side, rows, 2 * hc), F32),
            pltpu.VMEM((side, side, rows, hc), BF16),
            pltpu.VMEM((side, side, rows, hc), BF16),
            pltpu.VMEM((side, side, rows, hc), BF16),
            pltpu.VMEM((side, side, 1, LANES), F32),
            pltpu.VMEM((side, side, rows, 1), F32),
            pltpu.VMEM((2, side, side, rows, width), F32),
            pltpu.VMEM((2, 2, hop, side, rows, width), BF16),
            pltpu.VMEM((2, 2, hop + 1, side, rows, width), BF16),
            pltpu.VMEM((2, side, rows, width), BF16),
            pltpu.VMEM((2, side, rows, width), BF16),
            dma((12,)),
            dma((2, side)), dma((2, side)),
            dma((2, 2, hop, nb)), dma((2, side, nb)),
            dma((2, side)), dma((2, side)),
            dma((side,)), dma((side,)), dma((side,)), dma((side,)),
            dma((2,)), dma((2,)),
            dma((2, 2, hop, nb)), dma((2, 2, hop + 1, nb)),
            dma((2, side)), dma((2, side)),
        ]
        hbm = pl.BlockSpec(memory_space=pl.ANY)
        return pl.pallas_call(
            functools.partial(kernel, side, n_expert // experts),
            out_shape=jax.ShapeDtypeStruct((rows, 2 * width), BF16),
            in_specs=[hbm] * 5,
            out_specs=pl.BlockSpec(memory_space=pltpu.VMEM),
            scratch_shapes=scratch,
            compiler_params=pltpu.CompilerParams(
                collective_id=0, has_side_effects=True, vmem_limit_bytes=60 * 1024 * 1024
            ),
            name="moe_layer",
        )(tokens, wrow, gate_weight, up_weight, down_weight)

    return jax.shard_map(
        layer,
        mesh=mesh,
        in_specs=(
            P(("groups", "expert"), None),
            P(("groups", "expert"), None),
            P(("groups", "expert"), None),
            P("expert", None, "tensor"),
            P("expert", None, "tensor"),
            P("expert", "tensor", None),
        ),
        out_specs=P(("groups", "expert"), "tensor"),
        check_vma=False,
    )
```

time: 315 us -> 94.7 us (0.30)
  waiting for transfers between devices: 116 us -> 0 us
  blocking collectives: 99.9 us -> 0 us
  Pallas kernels: 0 us -> 89.8 us
  local copies, waits for them, and re-layouts: 35.5 us -> 2.03 us
  starting transfers between devices: 23.4 us -> 0 us
  between operations: 13.6 us -> 0.01 us
  other arithmetic: 13.1 us -> 1.47 us
  matrix products: 10.2 us -> 0 us
    all_to_all x2 -> x0, blocking collectives: 99.9 us -> none  [the longest x1 88.7 us: shards(): lax.all_to_all(own_columns, 'expert', split_axis=0, concat_axis=0, tiled=...]
    pallas_call x0 -> x1, Pallas kernels: none -> 89.8 us  [layer(): pl.pallas_call(functools.partial(kernel, side, n_expert // experts), out_...]
    all_to_all x2 -> x0, waiting for transfers between devices: 81.1 us -> none  [exchange_in_pieces(): lax.all_to_all(share, axis, split_axis=0, concat_axis=0, tiled=True)]
    all_gather x1 -> x0, waiting for transfers between devices: 35.1 us -> none  [shards(): lax.all_gather(lax.all_to_all(own_columns, 'expert', split_axis=0, concat...]
    all_to_all x2 -> x0, starting transfers between devices: 23.4 us -> none  [exchange_in_pieces(): lax.all_to_all(share, axis, split_axis=0, concat_axis=0, tiled=True)]
    dot_general x5 -> x0, matrix products: 10.2 us -> none  [the longest x1 3.44 us: shards(): jnp.dot(flattened, gate_local, preferred_element_type=jnp.float32)]
    split x4 -> x0, local copies, waits for them, and re-layouts: 9.65 us -> none  [exchange_in_pieces(): jnp.split(blocks, piece_ends(blocks.shape[widest], pieces), axis=widest)]
    reshape x4 -> x1, local copies, waits for them, and re-layouts: 9.6 us -> 0.09 us  [layer(): weight.T.reshape(1, experts * rows)]
  transfers between devices with their start and end apart: 3 -> 0, of which waited for: 3 -> 0; matrix products, arithmetic and copies ran while one was open for 5% -> 0% of each run, Pallas kernels for 0% -> 0%
where the time goes in v1:
time: 94.7 us; the launch traced here: 93.3 us
  Pallas kernels  89.8 us (95%)
  local copies, waits for them, and re-layouts  2.03 us (2%)
  other arithmetic  1.47 us (2%)
    pallas_call x1, Pallas kernels, layer(): pl.pallas_call(functools.partial(kernel, side, n_expert // experts), out_...  89.8 us

profile of v1, /device:TPU:513, one launch (start us, length us, event | category | flops | bytes accessed | tf_op | source)
XLA Modules:
  0.0 93.3 jit_solution(8057452072258600756)
XLA Ops:
  0.0 0.7 select_reduce_fusion.1
  0.8 0.7 select_reduce_fusion
  1.5 0.1 reshape.40
  1.6 0.5 pad.4.wrow
  2.1 89.8 %moe_layer.1 = bf16[8,3072]{1,0:T(8,128)(2,1)} custom-call(bf16[8,6144]{1,0:T(8,128)(2,1)} %tok.1, f32[1,128]{1,0:T(1,128)} %pad.4.wrow, bf16[1,6144,256]{2,1,0:T(8,128)(2,1)} %gate.1, bf16[1,6144,256]{2,1,0:T(8,128)(2,1)} %up.1, bf16[1,256,6144]{2,1,0:T(8,128)(2,1)} %down.1), custom_call_target="tpu_custom_call" | custom-call | tf_op jit(solution)/shard_map/moe_layer/pallas_call | solution.py:315
  91.9 1.4 %copy.10 = bf16[8,3072]{1,0:T(8,128)(2,1)} copy(bf16[8,3072]{1,0:T(8,128)(2,1)} %moe_layer.1) | data formatting | bytes 98304
  (3 shorter events, 0.1 us)

commit v2 on v1

--- a/solution.py
+++ b/solution.py
@@ -21,8 +21,8 @@
 
 
 def kernel(
-    side, segs, tok, wrow, gate, up, down, out,
-    gu, wd, own, sib, pre, hid, hmir, hsib, wall, wcol, part, csend, crecv, fsend, frecv,
+    side, segs, tok, routes, logits, gate, up, down, out,
+    named, scores, gu, wd, own, sib, pre, hid, hmir, hsib, wall, wcol, part, csend, crecv, fsend, frecv,
     load_sem, p1_send, p1_recv, ring_send, ring_recv, d2d_send, d2d_recv,
     w1_send, w1_recv, w2_send, w2_recv, x_send, x_recv,
     cr_send, cr_recv, f_send, f_recv,
@@ -30,7 +30,7 @@
     order = ring_order(side)
     pos = {k: p for p, k in enumerate(order)}
     mirror = [pos[(side - k) % side] for k in order]
-    cuts = [0, 1] + list(range(3, side - 2, 2)) + [side]
+    cuts = [0] + list(range(1, side, 2)) + [side]
     blocks = list(zip(cuts[:-1], cuts[1:]))
     nb = len(blocks)
     rows, width = own.shape[3], own.shape[4]
@@ -71,10 +71,12 @@
         )
         for t in range(2)
     ]
-    w_load = pltpu.make_async_copy(wrow, wall.at[0, 0], load_sem.at[2])
-    for copy in tok_loads:
+    small_loads = [
+        pltpu.make_async_copy(routes, named, load_sem.at[2]),
+        pltpu.make_async_copy(logits, scores, load_sem.at[12]),
+    ]
+    for copy in tok_loads + small_loads:
         copy.start()
-    w_load.start()
     loads = []
     for q in range(4):
         who = core if q < 2 else 1 - core
@@ -93,20 +95,22 @@
     wd_load.start()
 
     barrier = pltpu.get_barrier_semaphore()
-    for k in range(1, side):
+    for k in (1, side - 1):
         for axis in range(2):
             pl.semaphore_signal(barrier, inc=1, device_id=along(axis, k), device_id_type=MESH)
     pl.semaphore_signal(barrier, inc=1, device_id=other, device_id_type=MESH)
-    pre[...] = jnp.zeros_like(pre)
     for copy in tok_loads:
         copy.wait()
-    w_load.wait()
-    pl.semaphore_wait(barrier, 2 * (side - 1) + 1)
-
-    for k in order[1:]:
-        back = pos[side - k]
-        for t in range(2):
-            start(remote(own.at[t, 0, 0], own.at[t, 0, back], p1_send.at[t, back], p1_recv.at[t, back], along(t, k)))
+    pl.semaphore_wait(barrier, 5)
+
+    def pass_on(t, d, h):
+        k = (side - h) % side if d == 0 else h
+        k_there = side - h - 1 if d == 0 else h + 1
+        start(remote(
+            own.at[t, 0, pos[k]], own.at[t, 0, pos[k_there]],
+            p1_send.at[t, pos[k_there]], p1_recv.at[t, pos[k_there]], along(t, 1 if d == 0 else side - 1),
+        ))
+
     def forward(t, d, h, b):
         lo, hi = blocks[b]
         k = (side - h) % side if d == 0 else h
@@ -135,6 +139,13 @@
     loaded = False
     for step in range(side // 2 + nb):
         complete = []
+        for t in range(2):
+            for d in range(2):
+                if 0 < step <= hops[d]:
+                    p = pos[side - step if d == 0 else step]
+                    arrived(own.at[t, 0, p], p1_send.at[t, p], p1_recv.at[t, p])
+                if step < hops[d]:
+                    pass_on(t, d, step)
         for h in reversed(range(side // 2 + 1)):
             b = step - h
             if b < 0 or b >= nb:
@@ -142,8 +153,6 @@
             lo, hi = blocks[b]
             for t in range(2):
                 if h == 0:
-                    for p in range(max(lo, 1), hi):
-                        arrived(own.at[t, 0, p], p1_send.at[t, p], p1_recv.at[t, p])
                     for d in range(2):
                         forward(t, d, 0, b)
                     if b == nb - 1:
@@ -165,10 +174,26 @@
                 down.at[0, :, pl.ds(pl.multiple_of((1 - core) * half, LANES), half)], wd.at[1],
                 x_send.at[0], x_recv.at[0], other,
             ))
+            pre[...] = jnp.zeros_like(pre)
+            for copy in small_loads:
+                copy.wait()
+            experts = scores.shape[0]
+            picked = [
+                sum(jnp.where(named[k:k + 1, :] == e, scores[e:e + 1, :], 0.0) for e in range(experts)) for k in range(2)
+            ]
+            top = jnp.maximum(picked[0], picked[1])
+            raised = [jnp.exp(v - top) for v in picked]
+            weight = [v / (raised[0] + raised[1]) for v in raised]
+            wall[0, 0] = jnp.zeros_like(wall[0, 0])
+            for e in range(experts):
+                wall[0, 0, :, e * rows:(e + 1) * rows] = sum(
+                    jnp.where(named[k:k + 1, :] == e, weight[k], 0.0) for k in range(2)
+                )
+        if step == nb:
             for k in order[1:]:
                 back = pos[side - k]
                 start(remote(wall.at[0, 0], wall.at[0, back], w1_send.at[back], w1_recv.at[back], along(0, k)))
-        if step == nb - 1:
+        if step == side // 2 + nb - 1:
             for p in range(1, side):
                 arrived(wall.at[0, p], w1_send.at[p], w1_recv.at[p])
             for k in order[1:]:
@@ -224,43 +249,41 @@
             made.add((t, k))
             make_part(t, pos[k])
 
-    for step in range(side // 2 + nb):
-        for h in reversed(range(side // 2 + 1)):
-            b = step - h
-            if b < 0 or b >= nb:
-                continue
+    def handled(h):
+        return [(t, d, hops[d] - h if d == 0 else side - hops[d] + h) for t in range(2) for d in range(2) if h < hops[d]]
+
+    for h in range(side // 2):
+        for b in range(nb):
             lo, hi = back_blocks[b]
-            for t in range(2):
-                if h == side // 2:
-                    need(t, 0)
-                    arrived(crecv.at[t, 0, h, lo:hi], cr_send.at[t, 0, 0, b], cr_recv.at[t, 0, h, b])
-                    arrived(crecv.at[t, 1, h - 1, lo:hi], cr_send.at[t, 0, 0, b], cr_recv.at[t, 1, h - 1, b])
-                    total = (
-                        part[t, 0, lo:hi]
-                        + crecv[t, 0, h, lo:hi].astype(F32)
-                        + crecv[t, 1, h - 1, lo:hi].astype(F32)
-                    )
-                    part[t, 0, lo:hi] = total
-                    fsend[t, lo:hi] = total.astype(BF16)
-                    for p in reversed(range(max(lo, 1), hi)):
-                        k = order[p]
-                        back = pos[side - k]
-                        start(remote(fsend.at[t, p], frecv.at[t, back], f_send.at[t, back], f_recv.at[t, back], along(t, k)))
-                    continue
-                for d in range(2):
-                    if h >= hops[d]:
-                        continue
-                    k = hops[d] - h if d == 0 else side - hops[d] + h
-                    need(t, k)
-                    value = part[t, pos[k], lo:hi]
-                    if h > 0:
-                        arrived(crecv.at[t, d, h, lo:hi], cr_send.at[t, 0, 0, b], cr_recv.at[t, d, h, b])
-                        value = value + crecv[t, d, h, lo:hi].astype(F32)
-                    csend[t, d, h, lo:hi] = value.astype(BF16)
-                    start(remote(
-                        csend.at[t, d, h, lo:hi], crecv.at[t, d, h + 1, lo:hi],
-                        cr_send.at[t, d, h, b], cr_recv.at[t, d, h + 1, b], along(1 - t, 1 if d == 0 else side - 1),
-                    ))
+            for t, d, k in handled(h):
+                need(t, k)
+                value = part[t, pos[k], lo:hi]
+                if h > 0:
+                    arrived(crecv.at[t, d, h, lo:hi], cr_send.at[t, 0, 0, b], cr_recv.at[t, d, h, b])
+                    value = value + crecv[t, d, h, lo:hi].astype(F32)
+                csend[t, d, h, lo:hi] = value.astype(BF16)
+                start(remote(
+                    csend.at[t, d, h, lo:hi], crecv.at[t, d, h + 1, lo:hi],
+                    cr_send.at[t, d, h, b], cr_recv.at[t, d, h + 1, b], along(1 - t, 1 if d == 0 else side - 1),
+                ))
+        for t, _, k in handled(h + 1):
+            need(t, k)
+    for t in range(2):
+        need(t, 0)
+    for b in range(nb):
+        lo, hi = back_blocks[b]
+        for t in range(2):
+            total = part[t, 0, lo:hi]
+            for d in range(2):
+                arrived(crecv.at[t, d, hops[d], lo:hi], cr_send.at[t, 0, 0, b], cr_recv.at[t, d, hops[d], b])
+                total = total + crecv[t, d, hops[d], lo:hi].astype(F32)
+            part[t, 0, lo:hi] = total
+            fsend[t, lo:hi] = total.astype(BF16)
+            for p in reversed(range(max(lo, 1), hi)):
+                back = pos[side - order[p]]
+                start(remote(
+                    fsend.at[t, p], frecv.at[t, back], f_send.at[t, back], f_recv.at[t, back], along(t, order[p])
+                ))
     for t in range(2):
         total = part[t, 0, 0]
         for p in range(1, side):
@@ -274,19 +297,17 @@
 def solution(mesh):
     n_expert = mesh.shape["expert"]
     side = math.isqrt(n_expert)
-    nb = len([0, 1] + list(range(3, side - 2, 2)))
+    nb = side // 2 + 1
 
     def layer(tokens, routes, router_logits, gate_weight, up_weight, down_weight):
         rows, width = tokens.shape[0], tokens.shape[1] // 4
         experts = router_logits.shape[1]
         hc = down_weight.shape[1]
-        named = routes[:, :, None] == jnp.arange(experts, dtype=jnp.int32)
-        picked = jnp.sum(jnp.where(named, router_logits[:, None, :], 0.0), axis=2)
-        weight = jnp.sum(jnp.where(named, jax.nn.softmax(picked, axis=1)[:, :, None], 0.0), axis=1)
-        wrow = jnp.pad(weight.T.reshape(1, experts * rows), ((0, 0), (0, LANES - experts * rows)))
         hop = side // 2
         dma = pltpu.SemaphoreType.DMA
         scratch = [
+            pltpu.VMEM((routes.shape[1], rows), jnp.int32),
+            pltpu.VMEM((experts, rows), F32),
             pltpu.VMEM((4, width, 2 * hc), BF16),
             pltpu.VMEM((2, hc, 2 * width), BF16),
             pltpu.VMEM((2, side, side, rows, width), BF16),
@@ -302,7 +323,7 @@
             pltpu.VMEM((2, 2, hop + 1, side, rows, width), BF16),
             pltpu.VMEM((2, side, rows, width), BF16),
             pltpu.VMEM((2, side, rows, width), BF16),
-            dma((12,)),
+            dma((13,)),
             dma((2, side)), dma((2, side)),
             dma((2, 2, hop, nb)), dma((2, side, nb)),
             dma((2, side)), dma((2, side)),
@@ -315,14 +336,14 @@
         return pl.pallas_call(
             functools.partial(kernel, side, n_expert // experts),
             out_shape=jax.ShapeDtypeStruct((rows, 2 * width), BF16),
-            in_specs=[hbm] * 5,
+            in_specs=[hbm] * 6,
             out_specs=pl.BlockSpec(memory_space=pltpu.VMEM),
             scratch_shapes=scratch,
             compiler_params=pltpu.CompilerParams(
                 collective_id=0, has_side_effects=True, vmem_limit_bytes=60 * 1024 * 1024
             ),
             name="moe_layer",
-        )(tokens, wrow, gate_weight, up_weight, down_weight)
+        )(tokens, routes.T, router_logits.T, gate_weight, up_weight, down_weight)
 
     return jax.shard_map(
         layer,

time: 94.7 us -> 89.3 us (0.943); the launches traced: 93.3 us -> 89.1 us
  Pallas kernels: 89.8 us -> 87.7 us
  other arithmetic: 1.47 us -> 0 us
    pallas_call x1, Pallas kernels: 89.8 us -> 87.7 us  [layer(): pl.pallas_call(functools.partial(kernel, side, n_expert // experts), out_...]
    reduce_sum x3 -> x0, other arithmetic: 1.44 us -> none  [the longest x1 0.71 us: layer(): picked = jnp.sum(jnp.where(named, router_logits[:, None, :], 0.0), axis=2)]
where the time goes in v2:
time: 89.3 us; the launch traced here: 89.1 us
  Pallas kernels  87.7 us (98%)
  local copies, waits for them, and re-layouts  1.42 us (2%)
    pallas_call x1, Pallas kernels, layer(): pl.pallas_call(functools.partial(kernel, side, n_expert // experts), out_...  87.7 us

profile of v2, /device:TPU:513, one launch (start us, length us, event | category | flops | bytes accessed | tf_op | source)
XLA Modules:
  0.0 89.1 jit_solution(7470706384801319466)
XLA Ops:
  0.0 87.7 %moe_layer.1 = bf16[8,3072]{1,0:T(8,128)(2,1)} custom-call(bf16[8,6144]{1,0:T(8,128)(2,1)} %tok.1, s32[2,8]{1,0:T(2,128)} %bitcast.3, f32[4,8]{1,0:T(4,128)} %bitcast.2, bf16[1,6144,256]{2,1,0:T(8,128)(2,1)} %gate.1, bf16[1,6144,256]{2,1,0:T(8,128)(2,1)} %up.1, bf16[1,256,6144]{2,1,0:T(8,128)(2,1)} %down.1), custom_call_target="tpu_custom_call" | custom-call | tf_op jit(solution)/shard_map/moe_layer/pallas_call | solution.py:336
  87.7 1.4 %copy.8 = bf16[8,3072]{1,0:T(8,128)(2,1)} copy(bf16[8,3072]{1,0:T(8,128)(2,1)} %moe_layer.1) | data formatting | bytes 98304

commit v3 on v2

--- a/solution.py
+++ b/solution.py
@@ -30,12 +30,13 @@
     order = ring_order(side)
     pos = {k: p for p, k in enumerate(order)}
     mirror = [pos[(side - k) % side] for k in order]
-    cuts = [0] + list(range(1, side, 2)) + [side]
+    cuts = [0, 1] + list(range(3, side - 2, 2)) + [side]
     blocks = list(zip(cuts[:-1], cuts[1:]))
     nb = len(blocks)
     rows, width = own.shape[3], own.shape[4]
     hc = wd.shape[1]
     hops = (side // 2, side // 2 - 1)
+    x_pieces = x_send.shape[0] - 1
 
     core = lax.axis_index("tensor")
     place = lax.axis_index("expert")
@@ -95,21 +96,17 @@
     wd_load.start()
 
     barrier = pltpu.get_barrier_semaphore()
-    for k in (1, side - 1):
+    for k in range(1, side):
         for axis in range(2):
             pl.semaphore_signal(barrier, inc=1, device_id=along(axis, k), device_id_type=MESH)
     pl.semaphore_signal(barrier, inc=1, device_id=other, device_id_type=MESH)
     for copy in tok_loads:
         copy.wait()
-    pl.semaphore_wait(barrier, 5)
-
-    def pass_on(t, d, h):
-        k = (side - h) % side if d == 0 else h
-        k_there = side - h - 1 if d == 0 else h + 1
-        start(remote(
-            own.at[t, 0, pos[k]], own.at[t, 0, pos[k_there]],
-            p1_send.at[t, pos[k_there]], p1_recv.at[t, pos[k_there]], along(t, 1 if d == 0 else side - 1),
-        ))
+    pl.semaphore_wait(barrier, 2 * (side - 1) + 1)
+
+    def pass_on(t, k):
+        back = pos[side - k]
+        start(remote(own.at[t, 0, 0], own.at[t, 0, back], p1_send.at[t, back], p1_recv.at[t, back], along(t, k)))
 
     def forward(t, d, h, b):
         lo, hi = blocks[b]
@@ -132,48 +129,50 @@
         project(own, t, t, chunk, False)
 
     def sib_dot(t, chunk):
-        arrived(sib.at[t, chunk], d2d_send.at[t, chunk], d2d_recv.at[t, chunk])
+        for b, (lo, hi) in enumerate(blocks):
+            arrived(sib.at[t, chunk, lo:hi], d2d_send.at[t, chunk, b], d2d_recv.at[t, chunk, b])
         project(sib, t, 2 + t, chunk, True)
 
     waiting = []
     loaded = False
-    for step in range(side // 2 + nb):
-        complete = []
+    for h, b in [(h, b) for h in range(side // 2 + 1) for b in range(nb)]:
+        step = h * nb + b
+        complete, here = [], []
+        lo, hi = blocks[b]
         for t in range(2):
+            if step == 0:
+                pass_on(t, order[1])
+                pass_on(t, order[2])
             for d in range(2):
-                if 0 < step <= hops[d]:
-                    p = pos[side - step if d == 0 else step]
-                    arrived(own.at[t, 0, p], p1_send.at[t, p], p1_recv.at[t, p])
-                if step < hops[d]:
-                    pass_on(t, d, step)
-        for h in reversed(range(side // 2 + 1)):
-            b = step - h
-            if b < 0 or b >= nb:
-                continue
-            lo, hi = blocks[b]
-            for t in range(2):
-                if h == 0:
-                    for d in range(2):
-                        forward(t, d, 0, b)
-                    if b == nb - 1:
-                        complete.append((t, 0))
+                if h > hops[d]:
                     continue
-                for d in range(2):
-                    if h > hops[d]:
-                        continue
-                    chunk = pos[(side - h) % side if d == 0 else h]
+                chunk = pos[(side - h) % side if d == 0 else h]
+                if h > 0:
                     arrived(own.at[t, chunk, lo:hi], ring_send.at[t, 0, 0, b], ring_recv.at[t, chunk, b])
-                    if h < hops[d]:
-                        forward(t, d, h, b)
+                elif d == 0:
+                    for p in range(max(lo, 1), hi):
+                        arrived(own.at[t, 0, p], p1_send.at[t, p], p1_recv.at[t, p])
+                if h < hops[d]:
+                    forward(t, d, h, b)
+                if h > 0 or d == 0:
+                    here.append((t, chunk, b))
                     if b == nb - 1:
                         complete.append((t, chunk))
-        for t, chunk in complete:
-            start(remote(own.at[t, chunk], sib.at[t, chunk], d2d_send.at[t, chunk], d2d_recv.at[t, chunk], other))
+            if step == 0:
+                for k in order[3:]:
+                    pass_on(t, k)
+        for t, chunk, b in here:
+            lo, hi = blocks[b]
+            start(remote(
+                own.at[t, chunk, lo:hi], sib.at[t, chunk, lo:hi], d2d_send.at[t, chunk, b], d2d_recv.at[t, chunk, b], other
+            ))
+        if step < x_pieces:
+            span = half // x_pieces
+            start(remote(
+                down.at[0, :, pl.ds(pl.multiple_of((1 - core) * half + step * span, LANES), span)],
+                wd.at[1, :, step * span:(step + 1) * span], x_send.at[step], x_recv.at[step], other,
+            ))
         if step == 0:
-            start(remote(
-                down.at[0, :, pl.ds(pl.multiple_of((1 - core) * half, LANES), half)], wd.at[1],
-                x_send.at[0], x_recv.at[0], other,
-            ))
             pre[...] = jnp.zeros_like(pre)
             for copy in small_loads:
                 copy.wait()
@@ -193,21 +192,22 @@
             for k in order[1:]:
                 back = pos[side - k]
                 start(remote(wall.at[0, 0], wall.at[0, back], w1_send.at[back], w1_recv.at[back], along(0, k)))
-        if step == side // 2 + nb - 1:
+        if step == 2 * nb:
             for p in range(1, side):
                 arrived(wall.at[0, p], w1_send.at[p], w1_recv.at[p])
             for k in order[1:]:
                 back = pos[side - k]
                 start(remote(wall.at[0], wall.at[back], w2_send.at[back], w2_recv.at[back], along(1, k)))
-        if (complete or waiting) and not loaded:
+        if complete and not loaded:
             for copy in loads:
                 copy.wait()
             loaded = True
         for t, chunk in complete:
             own_dot(t, chunk)
-        for t, chunk in waiting:
-            sib_dot(t, chunk)
-        waiting = complete
+        if complete:
+            for t, chunk in waiting:
+                sib_dot(t, chunk)
+            waiting = complete
     for t, chunk in waiting:
         sib_dot(t, chunk)
 
@@ -217,7 +217,7 @@
         hid[i] = h_here
         for j in range(side):
             hmir[mirror[i], mirror[j]] = h_here[j]
-    start(remote(hmir, hsib, x_send.at[1], x_recv.at[1], other))
+    start(remote(hmir, hsib, x_send.at[x_pieces], x_recv.at[x_pieces], other))
 
     for p in range(1, side):
         arrived(wall.at[p], w2_send.at[p], w2_recv.at[p])
@@ -228,8 +228,10 @@
         wcol[i] = jnp.sum(jnp.where(lane == expert * rows + row, spread, 0.0), axis=2, keepdims=True)
 
     wd_load.wait()
-    arrived(wd.at[1], x_send.at[0], x_recv.at[0])
-    arrived(hsib, x_send.at[1], x_recv.at[1])
+    for i in range(x_pieces):
+        span = half // x_pieces
+        arrived(wd.at[1, :, i * span:(i + 1) * span], x_send.at[i], x_recv.at[i])
+    arrived(hsib, x_send.at[x_pieces], x_recv.at[x_pieces])
 
     def make_part(t, chunk):
         if t == 0:
@@ -297,13 +299,14 @@
 def solution(mesh):
     n_expert = mesh.shape["expert"]
     side = math.isqrt(n_expert)
-    nb = side // 2 + 1
+    nb = len([0, 1] + list(range(3, side - 2, 2)))
 
     def layer(tokens, routes, router_logits, gate_weight, up_weight, down_weight):
         rows, width = tokens.shape[0], tokens.shape[1] // 4
         experts = router_logits.shape[1]
         hc = down_weight.shape[1]
         hop = side // 2
+        pieces = math.gcd(2 * width // LANES, side)
         dma = pltpu.SemaphoreType.DMA
         scratch = [
             pltpu.VMEM((routes.shape[1], rows), jnp.int32),
@@ -326,9 +329,9 @@
             dma((13,)),
             dma((2, side)), dma((2, side)),
             dma((2, 2, hop, nb)), dma((2, side, nb)),
-            dma((2, side)), dma((2, side)),
+            dma((2, side, nb)), dma((2, side, nb)),
             dma((side,)), dma((side,)), dma((side,)), dma((side,)),
-            dma((2,)), dma((2,)),
+            dma((pieces + 1,)), dma((pieces + 1,)),
             dma((2, 2, hop, nb)), dma((2, 2, hop + 1, nb)),
             dma((2, side)), dma((2, side)),
         ]

time: 89.3 us -> 82.1 us (0.919)
  Pallas kernels: 87.7 us -> 80.5 us
    pallas_call x1, Pallas kernels: 87.7 us -> 80.5 us  [layer(): pl.pallas_call(functools.partial(kernel, side, n_expert // experts), out_...]
where the time goes in v3:
time: 82.1 us; the launch traced here: 82 us
  Pallas kernels  80.5 us (98%)
  local copies, waits for them, and re-layouts  1.42 us (2%)
    pallas_call x1, Pallas kernels, layer(): pl.pallas_call(functools.partial(kernel, side, n_expert // experts), out_...  80.5 us

profile of v3, /device:TPU:513, one launch (start us, length us, event | category | flops | bytes accessed | tf_op | source)
XLA Modules:
  0.0 82.0 jit_solution(15943315647278366713)
XLA Ops:
  0.0 80.5 %moe_layer.1 = bf16[8,3072]{1,0:T(8,128)(2,1)} custom-call(bf16[8,6144]{1,0:T(8,128)(2,1)} %tok.1, s32[2,8]{1,0:T(2,128)} %bitcast.3, f32[4,8]{1,0:T(4,128)} %bitcast.2, bf16[1,6144,256]{2,1,0:T(8,128)(2,1)} %gate.1, bf16[1,6144,256]{2,1,0:T(8,128)(2,1)} %up.1, bf16[1,256,6144]{2,1,0:T(8,128)(2,1)} %down.1), custom_call_target="tpu_custom_call" | custom-call | tf_op jit(solution)/shard_map/moe_layer/pallas_call | solution.py:339
  80.6 1.4 %copy.8 = bf16[8,3072]{1,0:T(8,128)(2,1)} copy(bf16[8,3072]{1,0:T(8,128)(2,1)} %moe_layer.1) | data formatting | bytes 98304

commit v4 on v3

--- a/solution.py
+++ b/solution.py
@@ -22,7 +22,7 @@
 
 def kernel(
     side, segs, tok, routes, logits, gate, up, down, out,
-    named, scores, gu, wd, own, sib, pre, hid, hmir, hsib, wall, wcol, part, csend, crecv, fsend, frecv,
+    named, scores, gu, wd, own, sib, pre, hid, hmir, wall, wcol, part, csend, crecv, fsend, frecv,
     load_sem, p1_send, p1_recv, ring_send, ring_recv, d2d_send, d2d_recv,
     w1_send, w1_recv, w2_send, w2_recv, x_send, x_recv,
     cr_send, cr_recv, f_send, f_recv,
@@ -34,7 +34,7 @@
     blocks = list(zip(cuts[:-1], cuts[1:]))
     nb = len(blocks)
     rows, width = own.shape[3], own.shape[4]
-    hc = wd.shape[1]
+    hc = wd.shape[0] // 2
     hops = (side // 2, side // 2 - 1)
     x_pieces = x_send.shape[0] - 1
 
@@ -91,7 +91,7 @@
     for copy in loads:
         copy.start()
     wd_load = pltpu.make_async_copy(
-        down.at[0, :, pl.ds(pl.multiple_of(core * half, LANES), half)], wd.at[0], load_sem.at[3]
+        down.at[0, :, pl.ds(pl.multiple_of(core * half, LANES), half)], wd.at[:hc], load_sem.at[3]
     )
     wd_load.start()
 
@@ -117,27 +117,33 @@
             ring_send.at[t, d, h, b], ring_recv.at[t, pos[k_there], b], along(1 - t, 1 if d == 0 else side - 1),
         ))
 
-    def project(src, t, q, chunk, mirrored):
-        r = jnp.dot(src[t, chunk].reshape(side * rows, width), gu[q], preferred_element_type=F32)
-        r = r.reshape(side, rows, 2 * hc)
-        for p in range(side):
-            at = (mirror[chunk], mirror[p]) if mirrored else (chunk, p)
-            i, j = at if t == 0 else at[::-1]
-            pre[i, j] += r[p]
-
-    def own_dot(t, chunk):
-        project(own, t, t, chunk, False)
-
-    def sib_dot(t, chunk):
-        for b, (lo, hi) in enumerate(blocks):
-            arrived(sib.at[t, chunk, lo:hi], d2d_send.at[t, chunk, b], d2d_recv.at[t, chunk, b])
-        project(sib, t, 2 + t, chunk, True)
-
-    waiting = []
-    loaded = False
+    def span_of(h):
+        return (0, 1) if h == 0 else (2 * h - 1, min(2 * h + 1, side))
+
+    def project(src, t, q, h, mirrored):
+        first, last = span_of(h)
+        r = jnp.dot(src[t, first:last].reshape((last - first) * side * rows, width), gu[q], preferred_element_type=F32)
+        r = r.reshape(last - first, side, rows, 2 * hc)
+        for c in range(first, last):
+            for p in range(side):
+                at = (mirror[c], mirror[p]) if mirrored else (c, p)
+                i, j = at if t == 0 else at[::-1]
+                pre[i, j] += r[c - first, p]
+
+    def own_dots(h):
+        for t in range(2):
+            project(own, t, t, h, False)
+
+    def sib_dots(h):
+        for t in range(2):
+            for chunk in range(*span_of(h)):
+                for b, (lo, hi) in enumerate(blocks):
+                    arrived(sib.at[t, chunk, lo:hi], d2d_send.at[t, chunk, b], d2d_recv.at[t, chunk, b])
+            project(sib, t, 2 + t, h, True)
+
     for h, b in [(h, b) for h in range(side // 2 + 1) for b in range(nb)]:
         step = h * nb + b
-        complete, here = [], []
+        here = []
         lo, hi = blocks[b]
         for t in range(2):
             if step == 0:
@@ -156,8 +162,6 @@
                     forward(t, d, h, b)
                 if h > 0 or d == 0:
                     here.append((t, chunk, b))
-                    if b == nb - 1:
-                        complete.append((t, chunk))
             if step == 0:
                 for k in order[3:]:
                     pass_on(t, k)
@@ -170,7 +174,7 @@
             span = half // x_pieces
             start(remote(
                 down.at[0, :, pl.ds(pl.multiple_of((1 - core) * half + step * span, LANES), span)],
-                wd.at[1, :, step * span:(step + 1) * span], x_send.at[step], x_recv.at[step], other,
+                wd.at[hc:, step * span:(step + 1) * span], x_send.at[step], x_recv.at[step], other,
             ))
         if step == 0:
             pre[...] = jnp.zeros_like(pre)
@@ -198,26 +202,22 @@
             for k in order[1:]:
                 back = pos[side - k]
                 start(remote(wall.at[0], wall.at[back], w2_send.at[back], w2_recv.at[back], along(1, k)))
-        if complete and not loaded:
+        if step == nb - 1:
             for copy in loads:
                 copy.wait()
-            loaded = True
-        for t, chunk in complete:
-            own_dot(t, chunk)
-        if complete:
-            for t, chunk in waiting:
-                sib_dot(t, chunk)
-            waiting = complete
-    for t, chunk in waiting:
-        sib_dot(t, chunk)
+        if b == nb - 1:
+            own_dots(h)
+        if b == 1 and h > 0:
+            sib_dots(h - 1)
+    sib_dots(side // 2)
 
     for i in range(side):
         g, u = pre[i, :, :, :hc], pre[i, :, :, hc:]
         h_here = (g / (1.0 + jnp.exp(-g)) * u).astype(BF16)
-        hid[i] = h_here
+        hid[i, :, :, :hc] = h_here
         for j in range(side):
             hmir[mirror[i], mirror[j]] = h_here[j]
-    start(remote(hmir, hsib, x_send.at[x_pieces], x_recv.at[x_pieces], other))
+    start(remote(hmir, hid.at[:, :, :, hc:], x_send.at[x_pieces], x_recv.at[x_pieces], other))
 
     for p in range(1, side):
         arrived(wall.at[p], w2_send.at[p], w2_recv.at[p])
@@ -230,35 +230,33 @@
     wd_load.wait()
     for i in range(x_pieces):
         span = half // x_pieces
-        arrived(wd.at[1, :, i * span:(i + 1) * span], x_send.at[i], x_recv.at[i])
-    arrived(hsib, x_send.at[x_pieces], x_recv.at[x_pieces])
-
-    def make_part(t, chunk):
+        arrived(wd.at[hc:, i * span:(i + 1) * span], x_send.at[i], x_recv.at[i])
+    arrived(hid.at[:, :, :, hc:], x_send.at[x_pieces], x_recv.at[x_pieces])
+
+    def make_parts(t, first):
+        a = hid[first:first + 2] if t == 0 else hid[:, first:first + 2]
+        r = jnp.dot(
+            a.reshape(2 * side * rows, 2 * hc), wd[:, t * width:(t + 1) * width], preferred_element_type=F32
+        )
         if t == 0:
-            a, b, scale = hid[chunk], hsib[chunk], wcol[chunk]
+            part[t, first:first + 2] = r.reshape(2, side, rows, width) * wcol[first:first + 2]
         else:
-            a, b, scale = hid[:, chunk], hsib[:, chunk], wcol[:, chunk]
-        cols = slice(t * width, (t + 1) * width)
-        r = jnp.dot(a.reshape(side * rows, hc), wd[0, :, cols], preferred_element_type=F32)
-        r += jnp.dot(b.reshape(side * rows, hc), wd[1, :, cols], preferred_element_type=F32)
-        part[t, chunk] = r.reshape(side, rows, width) * scale
+            r = r.reshape(side, 2, rows, width)
+            for c in range(2):
+                part[t, first + c] = r[:, c] * wcol[:, first + c]
 
     back_blocks = blocks[::-1]
-    made = set()
-
-    def need(t, k):
-        if (t, k) not in made:
-            made.add((t, k))
-            make_part(t, pos[k])
-
-    def handled(h):
-        return [(t, d, hops[d] - h if d == 0 else side - hops[d] + h) for t in range(2) for d in range(2) if h < hops[d]]
-
     for h in range(side // 2):
-        for b in range(nb):
+        first = side - 2 - 2 * h
+        halves = [(t, b) for t in range(2) for b in range(nb)] if h == 0 else [(t, b) for b in range(nb) for t in range(2)]
+        for t, b in halves:
+            if h == 0 and b == 0:
+                make_parts(t, first)
             lo, hi = back_blocks[b]
-            for t, d, k in handled(h):
-                need(t, k)
+            for d in range(2):
+                if h >= hops[d]:
+                    continue
+                k = hops[d] - h if d == 0 else side - hops[d] + h
                 value = part[t, pos[k], lo:hi]
                 if h > 0:
                     arrived(crecv.at[t, d, h, lo:hi], cr_send.at[t, 0, 0, b], cr_recv.at[t, d, h, b])
@@ -268,10 +266,9 @@
                     csend.at[t, d, h, lo:hi], crecv.at[t, d, h + 1, lo:hi],
                     cr_send.at[t, d, h, b], cr_recv.at[t, d, h + 1, b], along(1 - t, 1 if d == 0 else side - 1),
                 ))
-        for t, _, k in handled(h + 1):
-            need(t, k)
-    for t in range(2):
-        need(t, 0)
+        if h + 1 < side // 2:
+            for t in range(2):
+                make_parts(t, first - 2)
     for b in range(nb):
         lo, hi = back_blocks[b]
         for t in range(2):
@@ -312,12 +309,11 @@
             pltpu.VMEM((routes.shape[1], rows), jnp.int32),
             pltpu.VMEM((experts, rows), F32),
             pltpu.VMEM((4, width, 2 * hc), BF16),
-            pltpu.VMEM((2, hc, 2 * width), BF16),
+            pltpu.VMEM((2 * hc, 2 * width), BF16),
             pltpu.VMEM((2, side, side, rows, width), BF16),
             pltpu.VMEM((2, side, side, rows, width), BF16),
             pltpu.VMEM((side, side, rows, 2 * hc), F32),
-            pltpu.VMEM((side, side, rows, hc), BF16),
-            pltpu.VMEM((side, side, rows, hc), BF16),
+            pltpu.VMEM((side, side, rows, 2 * hc), BF16),
             pltpu.VMEM((side, side, rows, hc), BF16),
             pltpu.VMEM((side, side, 1, LANES), F32),
             pltpu.VMEM((side, side, rows, 1), F32),

time: 82.1 us -> 78 us (0.950)
  Pallas kernels: 80.5 us -> 76.4 us
    pallas_call x1, Pallas kernels: 80.5 us -> 76.4 us  [layer(): pl.pallas_call(functools.partial(kernel, side, n_expert // experts), out_...]
where the time goes in v4:
time: 78 us; the launch traced here: 77.8 us
  Pallas kernels  76.4 us (98%)
  local copies, waits for them, and re-layouts  1.42 us (2%)
    pallas_call x1, Pallas kernels, layer(): pl.pallas_call(functools.partial(kernel, side, n_expert // experts), out_...  76.4 us

profile of v4, /device:TPU:513, one launch (start us, length us, event | category | flops | bytes accessed | tf_op | source)
XLA Modules:
  0.0 77.8 jit_solution(3904647455776074888)
XLA Ops:
  0.0 76.4 %moe_layer.1 = bf16[8,3072]{1,0:T(8,128)(2,1)} custom-call(bf16[8,6144]{1,0:T(8,128)(2,1)} %tok.1, s32[2,8]{1,0:T(2,128)} %bitcast.3, f32[4,8]{1,0:T(4,128)} %bitcast.2, bf16[1,6144,256]{2,1,0:T(8,128)(2,1)} %gate.1, bf16[1,6144,256]{2,1,0:T(8,128)(2,1)} %up.1, bf16[1,256,6144]{2,1,0:T(8,128)(2,1)} %down.1), custom_call_target="tpu_custom_call" | custom-call | tf_op jit(solution)/shard_map/moe_layer/pallas_call | solution.py:335
  76.4 1.4 %copy.8 = bf16[8,3072]{1,0:T(8,128)(2,1)} copy(bf16[8,3072]{1,0:T(8,128)(2,1)} %moe_layer.1) | data formatting | bytes 98304

commit v5 on v4

--- a/solution.py
+++ b/solution.py
@@ -36,7 +36,7 @@
     rows, width = own.shape[3], own.shape[4]
     hc = wd.shape[0] // 2
     hops = (side // 2, side // 2 - 1)
-    x_pieces = x_send.shape[0] - 1
+    x_pieces = x_send.shape[0] - side
 
     core = lax.axis_index("tensor")
     place = lax.axis_index("expert")
@@ -88,8 +88,6 @@
                     matrix.at[0, pl.ds(first, width), :], gu.at[q, :, pl.ds(i * hc, hc)], load_sem.at[4 + 2 * q + i]
                 )
             )
-    for copy in loads:
-        copy.start()
     wd_load = pltpu.make_async_copy(
         down.at[0, :, pl.ds(pl.multiple_of(core * half, LANES), half)], wd.at[:hc], load_sem.at[3]
     )
@@ -177,6 +175,8 @@
                 wd.at[hc:, step * span:(step + 1) * span], x_send.at[step], x_recv.at[step], other,
             ))
         if step == 0:
+            for copy in loads:
+                copy.start()
             pre[...] = jnp.zeros_like(pre)
             for copy in small_loads:
                 copy.wait()
@@ -202,22 +202,28 @@
             for k in order[1:]:
                 back = pos[side - k]
                 start(remote(wall.at[0], wall.at[back], w2_send.at[back], w2_recv.at[back], along(1, k)))
-        if step == nb - 1:
+        if h == 1 and b == 1:
             for copy in loads:
                 copy.wait()
-        if b == nb - 1:
-            own_dots(h)
-        if b == 1 and h > 0:
+        if h > 0 and b == 1:
+            own_dots(h - 1)
+        if h > 0 and b == min(2, nb - 1):
             sib_dots(h - 1)
+    own_dots(side // 2)
     sib_dots(side // 2)
 
-    for i in range(side):
+    for i in reversed(range(side)):
         g, u = pre[i, :, :, :hc], pre[i, :, :, hc:]
         h_here = (g / (1.0 + jnp.exp(-g)) * u).astype(BF16)
         hid[i, :, :, :hc] = h_here
         for j in range(side):
             hmir[mirror[i], mirror[j]] = h_here[j]
-    start(remote(hmir, hid.at[:, :, :, hc:], x_send.at[x_pieces], x_recv.at[x_pieces], other))
+        m = mirror[i]
+        start(remote(hmir.at[m], hid.at[m, :, :, hc:], x_send.at[x_pieces + m], x_recv.at[x_pieces + m], other))
+
+    def other_hidden(first, last):
+        for i in range(first, last):
+            arrived(hid.at[i, :, :, hc:], x_send.at[x_pieces + i], x_recv.at[x_pieces + i])
 
     for p in range(1, side):
         arrived(wall.at[p], w2_send.at[p], w2_recv.at[p])
@@ -231,7 +237,6 @@
     for i in range(x_pieces):
         span = half // x_pieces
         arrived(wd.at[hc:, i * span:(i + 1) * span], x_send.at[i], x_recv.at[i])
-    arrived(hid.at[:, :, :, hc:], x_send.at[x_pieces], x_recv.at[x_pieces])
 
     def make_parts(t, first):
         a = hid[first:first + 2] if t == 0 else hid[:, first:first + 2]
@@ -251,6 +256,7 @@
         halves = [(t, b) for t in range(2) for b in range(nb)] if h == 0 else [(t, b) for b in range(nb) for t in range(2)]
         for t, b in halves:
             if h == 0 and b == 0:
+                other_hidden(*((first, side) if t == 0 else (0, first)))
                 make_parts(t, first)
             lo, hi = back_blocks[b]
             for d in range(2):
@@ -327,7 +333,7 @@
             dma((2, 2, hop, nb)), dma((2, side, nb)),
             dma((2, side, nb)), dma((2, side, nb)),
             dma((side,)), dma((side,)), dma((side,)), dma((side,)),
-            dma((pieces + 1,)), dma((pieces + 1,)),
+            dma((pieces + side,)), dma((pieces + side,)),
             dma((2, 2, hop, nb)), dma((2, 2, hop + 1, nb)),
             dma((2, side)), dma((2, side)),
         ]

time: 78 us -> 77.4 us (level)
  no operation moved by 1% of the time
where the time goes in v5:
time: 77.4 us; the launch traced here: 77.3 us
  Pallas kernels  75.9 us (98%)
  local copies, waits for them, and re-layouts  1.42 us (2%)
    pallas_call x1, Pallas kernels, layer(): pl.pallas_call(functools.partial(kernel, side, n_expert // experts), out_...  75.9 us

profile of v5, /device:TPU:513, one launch (start us, length us, event | category | flops | bytes accessed | tf_op | source)
XLA Modules:
  0.0 77.3 jit_solution(12297799116188208022)
XLA Ops:
  0.0 75.9 %moe_layer.1 = bf16[8,3072]{1,0:T(8,128)(2,1)} custom-call(bf16[8,6144]{1,0:T(8,128)(2,1)} %tok.1, s32[2,8]{1,0:T(2,128)} %bitcast.3, f32[4,8]{1,0:T(4,128)} %bitcast.2, bf16[1,6144,256]{2,1,0:T(8,128)(2,1)} %gate.1, bf16[1,6144,256]{2,1,0:T(8,128)(2,1)} %up.1, bf16[1,256,6144]{2,1,0:T(8,128)(2,1)} %down.1), custom_call_target="tpu_custom_call" | custom-call | tf_op jit(solution)/shard_map/moe_layer/pallas_call | solution.py:341
  75.9 1.4 %copy.8 = bf16[8,3072]{1,0:T(8,128)(2,1)} copy(bf16[8,3072]{1,0:T(8,128)(2,1)} %moe_layer.1) | data formatting | bytes 98304

commit v6 on v5

--- a/solution.py
+++ b/solution.py
@@ -251,7 +251,9 @@
                 part[t, first + c] = r[:, c] * wcol[:, first + c]
 
     back_blocks = blocks[::-1]
+    drained = 0
     for h in range(side // 2):
+        before = len(started)
         first = side - 2 - 2 * h
         halves = [(t, b) for t in range(2) for b in range(nb)] if h == 0 else [(t, b) for b in range(nb) for t in range(2)]
         for t, b in halves:
@@ -275,6 +277,9 @@
         if h + 1 < side // 2:
             for t in range(2):
                 make_parts(t, first - 2)
+        for copy in started[drained:before]:
+            copy.wait_send()
+        drained = before
     for b in range(nb):
         lo, hi = back_blocks[b]
         for t in range(2):
@@ -295,7 +300,7 @@
             arrived(frecv.at[t, p], f_send.at[t, p], f_recv.at[t, p])
             total = total + frecv[t, p].astype(F32)
         out[:, t * width:(t + 1) * width] = total.astype(out.dtype)
-    for copy in started:
+    for copy in started[drained:]:
         copy.wait_send()
 
 

time: 77.4 us -> 77.1 us (level)
  no operation moved by 1% of the time
where the time goes in v6:
time: 77.1 us; the launch traced here: 77 us
  Pallas kernels  75.5 us (98%)
  local copies, waits for them, and re-layouts  1.42 us (2%)
    pallas_call x1, Pallas kernels, layer(): pl.pallas_call(functools.partial(kernel, side, n_expert // experts), out_...  75.5 us

profile of v6, /device:TPU:513, one launch (start us, length us, event | category | flops | bytes accessed | tf_op | source)
XLA Modules:
  0.0 77.0 jit_solution(9410452371087501466)
XLA Ops:
  0.0 75.5 %moe_layer.1 = bf16[8,3072]{1,0:T(8,128)(2,1)} custom-call(bf16[8,6144]{1,0:T(8,128)(2,1)} %tok.1, s32[2,8]{1,0:T(2,128)} %bitcast.3, f32[4,8]{1,0:T(4,128)} %bitcast.2, bf16[1,6144,256]{2,1,0:T(8,128)(2,1)} %gate.1, bf16[1,6144,256]{2,1,0:T(8,128)(2,1)} %up.1, bf16[1,256,6144]{2,1,0:T(8,128)(2,1)} %down.1), custom_call_target="tpu_custom_call" | custom-call | tf_op jit(solution)/shard_map/moe_layer/pallas_call | solution.py:346
  75.6 1.4 %copy.8 = bf16[8,3072]{1,0:T(8,128)(2,1)} copy(bf16[8,3072]{1,0:T(8,128)(2,1)} %moe_layer.1) | data formatting | bytes 98304
